TPU v7x, 32 devices: a whole 2x2x4 slice. The times are simulated.
32 devices in a mesh: dp: 4 (over y, x), samp: 4 (over z), col: 2 (over core).
Axes of the slice: x: 2, y: 2, z: 4, core: 2. Of those that a mesh axis runs over, the one named last changes fastest.
Arguments:
- looked_rows: bfloat16 [16, 1920, 128], P(('dp', 'samp'), None, 'col'), may hold values from -6 to 6
- bag_ids: int32 [16, 1920], P(('dp', 'samp')), may hold values from 0 to 959, never falling along the last dimension, each value on 1 to 4 neighbouring positions
- slot_of: int32 [40], replicated, may hold values from 0 to 39, each once
- labels: int32 [384], P(('dp', 'samp')), may hold values 0 or 1
- out_weight: bfloat16 [3, 128], replicated, may hold values from -0.02734375 to 0.02734375
- filter_first: bfloat16 [128, 1521], replicated, may hold values from -0.15625 to 0.15625
- filter_second: bfloat16 [128, 4992], replicated, may hold values from -0.078125 to 0.078125
- filter_third: bfloat16 [128, 4992], replicated, may hold values from -0.078125 to 0.078125
Outputs:
- row_grads: bfloat16 [16, 1920, 128], P(('dp', 'samp'), None, 'col')
- grad_first: float32 [128, 1521], P('dp')
- grad_second: float32 [128, 4992], P('dp')
- grad_third: float32 [128, 4992], P('dp')
Inputs may be any that keep to these rules, and one draw needn't show every extreme that they name: `bag_ids`: within each owner's row, bag numbers never fall; each of the 960 bags has 1 to 4 entries and some bag exactly 4. `slot_of`: each slot number once.
All inputs are finite; a program needn't handle non-finite values. No bound on the sum of `labels` on one device may be relied on, other than what follows from the above.
Results may differ from a plain program's by a relative error of at most 0.014.
Values may be sent and summed in bfloat16 or wider, within the bound.
No kernel may reach another device: no remote copies, remote signals or barrier semaphores. Data moves between devices by JAX's collectives and lax.ppermute only.
A program may use at most 64 MiB of HBM per device.

v0:
```python
import jax
import jax.numpy as jnp
from jax import lax
from jax.sharding import PartitionSpec as P

FIELDS = 39
loss_scale = 16.0
block_rows = 4


def outer_block(previous, anchor):
    spread_rows = previous.astype(jnp.float32)[:, None, :] * anchor.astype(jnp.float32)[None, :, :]
    return spread_rows.astype(jnp.bfloat16)


def forward_layer(filter_cube, previous, anchor):

    def one_block(operands):
        outer_products = outer_block(operands[0], operands[1])
        projected_maps = jnp.einsum(
            "ocf,cfl->ol", filter_cube, outer_products, preferred_element_type=jnp.float32
        )
        return projected_maps.astype(jnp.bfloat16)

    return lax.map(one_block, (previous, anchor))


def backward_layer(filter_cube, cotangent, previous, anchor):

    def accumulate(running, operands):
        cotangent_part, previous_block, anchor_block = operands
        outer_products = outer_block(previous_block, anchor_block)
        running = running + jnp.einsum(
            "ol,cfl->ocf", cotangent_part, outer_products, preferred_element_type=jnp.float32
        )
        spread_rows = jnp.einsum(
            "ocf,ol->cfl", filter_cube, cotangent_part, preferred_element_type=jnp.float32
        )
        grad_previous = jnp.sum(spread_rows * anchor_block.astype(jnp.float32)[None, :, :], axis=1)
        grad_anchor = jnp.sum(spread_rows * previous_block.astype(jnp.float32)[:, None, :], axis=0)
        return (running, (grad_previous, grad_anchor))

    starting = jnp.zeros(filter_cube.shape, jnp.float32)
    running, (grad_previous, grad_anchor) = lax.scan(
        accumulate, starting, (cotangent, previous, anchor)
    )
    return (
        running.reshape(filter_cube.shape[0], filter_cube.shape[1] * filter_cube.shape[2]),
        grad_previous,
        grad_anchor,
    )


def local(
    looked_rows, bag_ids, slot_of, labels, out_weight, filter_first, filter_second, filter_third
):
    samples = labels.shape[0]
    slots = slot_of.shape[0]
    bag_count = samples * slots
    owners = lax.axis_size("samp")
    group_size = samples * owners
    slot_span = slots // owners
    blocks = samples // block_rows
    entries = bag_ids[0]
    member = (entries[None, :] == jnp.arange(bag_count, dtype=jnp.int32)[:, None]).astype(
        jnp.bfloat16
    )
    pooled = jnp.dot(member, looked_rows[0], preferred_element_type=jnp.float32).astype(
        jnp.bfloat16
    )
    width = pooled.shape[1]
    lanes = block_rows * width
    pooled = pooled.reshape(group_size, slot_span, width)
    arrived = lax.all_to_all(pooled, "samp", split_axis=0, concat_axis=1, tiled=True)
    chooser = (slot_of[:FIELDS][:, None] == jnp.arange(slots, dtype=jnp.int32)[None, :]).astype(
        jnp.bfloat16
    )
    arrived_blocks = arrived.reshape(blocks, block_rows, slots, width)
    anchor = jnp.einsum(
        "fk,nbkd->nfbd", chooser, arrived_blocks, preferred_element_type=jnp.float32
    ).astype(jnp.bfloat16)
    anchor = anchor.reshape(blocks, FIELDS, lanes)
    cube_first = filter_first.reshape(filter_first.shape[0], FIELDS, FIELDS)
    cube_second = filter_second.reshape(
        filter_second.shape[0], filter_second.shape[1] // FIELDS, FIELDS
    )
    cube_third = filter_third.reshape(
        filter_third.shape[0], filter_third.shape[1] // FIELDS, FIELDS
    )
    maps_count = filter_first.shape[0]
    layer_one = forward_layer(cube_first, anchor, anchor)
    layer_two = forward_layer(cube_second, layer_one, anchor)
    layer_three = forward_layer(cube_third, layer_two, anchor)

    def column_sums(layer):
        summed = jnp.sum(
            layer.astype(jnp.float32).reshape(blocks, maps_count, block_rows, width), axis=3
        )
        return summed.transpose(0, 2, 1).reshape(samples, maps_count)

    maps_one, maps_two, maps_three = lax.psum(
        (column_sums(layer_one), column_sums(layer_two), column_sums(layer_three)), "col"
    )
    weights_out = out_weight.astype(jnp.float32)
    logits = jnp.dot(maps_one, weights_out[0], precision=lax.Precision.HIGHEST)
    logits = logits + jnp.dot(maps_two, weights_out[1], precision=lax.Precision.HIGHEST)
    logits = logits + jnp.dot(maps_three, weights_out[2], precision=lax.Precision.HIGHEST)
    residual_slope = loss_scale * (jax.nn.sigmoid(logits) - labels.astype(jnp.float32))

    def direct_term(weight_row):
        scaled = (residual_slope[:, None] * weight_row[None, :]).reshape(
            blocks, block_rows, maps_count
        )
        scaled = scaled.transpose(0, 2, 1)[:, :, :, None]
        return jnp.broadcast_to(scaled, (blocks, maps_count, block_rows, width)).reshape(
            blocks, maps_count, lanes
        )

    cotan_three = direct_term(weights_out[2]).astype(jnp.bfloat16)
    grad_three, back_two, base_three = backward_layer(cube_third, cotan_three, layer_two, anchor)
    cotan_two = (direct_term(weights_out[1]) + back_two).astype(jnp.bfloat16)
    grad_two, back_one, base_two = backward_layer(cube_second, cotan_two, layer_one, anchor)
    cotan_one = (direct_term(weights_out[0]) + back_one).astype(jnp.bfloat16)
    grad_one, back_zero, base_one = backward_layer(cube_first, cotan_one, anchor, anchor)
    grad_fields = (back_zero + base_one + base_two + base_three).astype(jnp.bfloat16)
    grad_fields = grad_fields.reshape(blocks, FIELDS, block_rows, width)
    slot_grads = jnp.einsum(
        "fk,nfbd->nbkd", chooser, grad_fields, preferred_element_type=jnp.float32
    ).astype(jnp.bfloat16)
    slot_grads = slot_grads.reshape(samples, slots, width)
    returned = lax.all_to_all(slot_grads, "samp", split_axis=1, concat_axis=0, tiled=True)
    bag_grads = returned.reshape(bag_count, width)
    row_grads = jnp.einsum(
        "be,bd->ed", member, bag_grads, preferred_element_type=jnp.float32
    ).astype(jnp.bfloat16)
    shares = (
        lax.psum_scatter(
            grad_one.astype(jnp.bfloat16), "dp", scatter_dimension=0, tiled=True
        ).astype(jnp.float32),
        lax.psum_scatter(
            grad_two.astype(jnp.bfloat16), "dp", scatter_dimension=0, tiled=True
        ).astype(jnp.float32),
        lax.psum_scatter(
            grad_three.astype(jnp.bfloat16), "dp", scatter_dimension=0, tiled=True
        ).astype(jnp.float32),
    )
    summed = (
        lax.psum(shares[0].astype(jnp.bfloat16), ("samp", "col")).astype(jnp.float32),
        lax.psum(shares[1].astype(jnp.bfloat16), ("samp", "col")).astype(jnp.float32),
        lax.psum(shares[2].astype(jnp.bfloat16), ("samp", "col")).astype(jnp.float32),
    )
    return (row_grads[None], summed[0], summed[1], summed[2])


def solution(mesh):
    in_specs = (
        P(("dp", "samp"), None, "col"),
        P(("dp", "samp"), None),
        P(),
        P(("dp", "samp")),
        P(),
        P(),
        P(),
        P(),
    )
    out_specs = (P(("dp", "samp"), None, "col"), P("dp", None), P("dp", None), P("dp", None))
    return jax.shard_map(local, mesh=mesh, in_specs=in_specs, out_specs=out_specs, check_vma=False)
```

profile of v0, /device:TPU:0, one launch (start us, length us, event | category | flops | bytes accessed | tf_op | source)
XLA Modules:
  0.0 423.8 jit_solution(5831816907563971014)
XLA Ops:
  10.8 6.3 %all-to-all-start = ((bf16[4,2,7680]{2,1,0:T(2,128)(2,1)}), bf16[4,2,7680]{2,1,0:T(2,128)(2,1)S(1)}, u32[]{:S(2)}, u32[]{:S(2)}) async-start(bf16[4,2,7680]{2,1,0:T(2,128)(2,1)} %reshape.218), calls=%async_computation | async-start | bytes 245760 | tf_op jit(solution)/shard_map/all_to_all | solution.py:74
  32.3 9.0 %while.75 = (s32[]{:T(128)}, bf16[6,128,256]{1,2,0:T(8,128)(2,1)S(1)}, bf16[6,39,256]{2,1,0:T(8,128)(2,1)S(1)}, bf16[128,39,39]{0,2,1:T(8,128)(2,1)}, s32[]{:T(128)}) while((s32[]{:T(128)}, bf16[6,128,256]{1,2,0:T(8,128)(2,1)S(1)}, bf16[6,39,256]{2,1,0:T(8,128)(2,1)S(1)}, bf16[128,39,39]{0,2,1:T(8,128)(2,1)}, s32[]{:T(128)}) %tuple.131), condition=%wide.region_1.2_spmd, body=%wide.region_0.1_spmd.sunk | while | flops 100501760 | bytes 596805 | solution.py:25
  42.2 20.9 %while.76 = (s32[]{:T(128)}, bf16[6,128,256]{1,2,0:T(8,128)(2,1)}, bf16[6,128,256]{1,2,0:T(8,128)(2,1)S(1)}, bf16[6,39,256]{2,1,0:T(8,128)(2,1)S(1)}, bf16[128,128,39]{1,0,2:T(8,128)(2,1)}, /*index=5*/s32[]{:T(128)}) while((s32[]{:T(128)}, bf16[6,128,256]{1,2,0:T(8,128)(2,1)}, bf16[6,128,256]{1,2,0:T(8,128)(2,1)S(1)}, ...), condition=%wide.region_5.6_spmd, body=%wide.region_4.5_spmd.sunk | while | flops 329787136 | bytes 1771597 | solution.py:25
  42.2 3.5 fusion.114
  45.7 3.5 fusion.114
  49.2 3.5 fusion.114
  52.7 3.5 fusion.114
  56.2 3.5 fusion.114
  59.6 3.5 fusion.114
  65.0 25.9 %while.77 = (s32[]{:T(128)}, bf16[6,128,256]{1,2,0:T(8,128)(2,1)}, bf16[6,128,256]{1,2,0:T(8,128)(2,1)}, bf16[6,39,256]{2,1,0:T(8,128)(2,1)S(1)}, bf16[128,128,39]{1,0,2:T(8,128)(2,1)}, /*index=5*/s32[]{:T(128)}) while((s32[]{:T(128)}, bf16[6,128,256]{1,2,0:T(8,128)(2,1)}, bf16[6,128,256]{1,2,0:T(8,128)(2,1)}, ...), condition=%wide.region_9.10_spmd, body=%wide.region_8.9_spmd.sunk | while | flops 329787136 | bytes 1771597 | solution.py:25
  65.9 3.5 fusion.116
  70.2 3.4 fusion.116
  74.5 3.4 fusion.116
  78.8 3.4 fusion.116
  83.2 3.5 fusion.116
  87.5 3.4 fusion.116
  92.0 3.7 all-reduce
  99.4 60.1 %while.78 = (s32[]{:T(128)}, f32[128,128,39]{1,0,2:T(8,128)}, f32[6,128,256]{1,2,0:T(8,128)}, f32[6,39,256]{2,1,0:T(8,128)}, bf16[6,128,256]{1,2,0:T(8,128)(2,1)...) while((s32[]{:T(128)}, f32[128,128,39]{1,0,2:T(8,128)}, ...), condition=%wide.region_15.16_spmd.clone, body=%wide.region_12.15_spmd.clone.sunk | while | flops 663257088 | bytes 13271699 | solution.py:44
  100.4 3.4 select_add_fusion.4
  103.8 2.5 fusion.119
  109.7 4.3 %select_add_fusion.4 = f32[128,128,39]{1,0,2:T(8,128)} fusion(f32[128,128,39]{1,0,2:T(8,128)} %get-tuple-element.797, f32[39,256]{1,0:T(8,128)S(1)} %bitcast_convert_fusion.25, f32[128,256]{1,0:T(8,128)S(1)} %bitcast_convert_fusion.26, pred[]{:T(512)S(6)} %compare.9, bf16[6,128,256]{1,2,0:T(8,128)(2,1)} %get-tuple-element.810, s32[]{:T(128)} %get-tuple-element.796), kind=kOutput, calls=%fused_computation.34.clone.1 | convolution fusion | flops 330989568 | bytes 5348865 | tf_op jit(solution)/shard_map/while/body/eval_jaxpr/ol,cfl->ocf/dot_general | solution.py:33
  114.0 2.5 fusion.119
  119.8 4.3 %select_add_fusion.4 = f32[128,128,39]{1,0,2:T(8,128)} fusion(f32[128,128,39]{1,0,2:T(8,128)} %get-tuple-element.797, f32[39,256]{1,0:T(8,128)S(1)} %bitcast_convert_fusion.25, f32[128,256]{1,0:T(8,128)S(1)} %bitcast_convert_fusion.26, pred[]{:T(512)S(6)} %compare.9, bf16[6,128,256]{1,2,0:T(8,128)(2,1)} %get-tuple-element.810, s32[]{:T(128)} %get-tuple-element.796), kind=kOutput, calls=%fused_computation.34.clone.1 | convolution fusion | flops 330989568 | bytes 5348865 | tf_op jit(solution)/shard_map/while/body/eval_jaxpr/ol,cfl->ocf/dot_general | solution.py:33
  124.2 2.5 fusion.119
  130.0 4.3 %select_add_fusion.4 = f32[128,128,39]{1,0,2:T(8,128)} fusion(f32[128,128,39]{1,0,2:T(8,128)} %get-tuple-element.797, f32[39,256]{1,0:T(8,128)S(1)} %bitcast_convert_fusion.25, f32[128,256]{1,0:T(8,128)S(1)} %bitcast_convert_fusion.26, pred[]{:T(512)S(6)} %compare.9, bf16[6,128,256]{1,2,0:T(8,128)(2,1)} %get-tuple-element.810, s32[]{:T(128)} %get-tuple-element.796), kind=kOutput, calls=%fused_computation.34.clone.1 | convolution fusion | flops 330989568 | bytes 5348865 | tf_op jit(solution)/shard_map/while/body/eval_jaxpr/ol,cfl->ocf/dot_general | solution.py:33
  134.3 2.5 fusion.119
  140.2 4.3 %select_add_fusion.4 = f32[128,128,39]{1,0,2:T(8,128)} fusion(f32[128,128,39]{1,0,2:T(8,128)} %get-tuple-element.797, f32[39,256]{1,0:T(8,128)S(1)} %bitcast_convert_fusion.25, f32[128,256]{1,0:T(8,128)S(1)} %bitcast_convert_fusion.26, pred[]{:T(512)S(6)} %compare.9, bf16[6,128,256]{1,2,0:T(8,128)(2,1)} %get-tuple-element.810, s32[]{:T(128)} %get-tuple-element.796), kind=kOutput, calls=%fused_computation.34.clone.1 | convolution fusion | flops 330989568 | bytes 5348865 | tf_op jit(solution)/shard_map/while/body/eval_jaxpr/ol,cfl->ocf/dot_general | solution.py:33
  150.3 4.3 %select_add_fusion.4 = f32[128,128,39]{1,0,2:T(8,128)} fusion(f32[128,128,39]{1,0,2:T(8,128)} %get-tuple-element.797, f32[39,256]{1,0:T(8,128)S(1)} %bitcast_convert_fusion.25, f32[128,256]{1,0:T(8,128)S(1)} %bitcast_convert_fusion.26, pred[]{:T(512)S(6)} %compare.9, bf16[6,128,256]{1,2,0:T(8,128)(2,1)} %get-tuple-element.810, s32[]{:T(128)} %get-tuple-element.796), kind=kOutput, calls=%fused_computation.34.clone.1 | convolution fusion | flops 330989568 | bytes 5348865 | tf_op jit(solution)/shard_map/while/body/eval_jaxpr/ol,cfl->ocf/dot_general | solution.py:33
  163.1 46.5 %while.79 = (s32[]{:T(128)}, f32[128,128,39]{1,0,2:T(8,128)S(1)}, f32[6,128,256]{1,2,0:T(8,128)}, f32[6,39,256]{2,1,0:T(8,128)}, bf16[6,128,256]{1,2,0:T(8,128)(...) while((s32[]{:T(128)}, f32[128,128,39]{1,0,2:T(8,128)S(1)}, ...), condition=%wide.region_19.20_spmd.clone, body=%wide.region_16.19_spmd.clone.sunk | while | flops 663257088 | bytes 13271699 | solution.py:44
  163.3 2.7 select_add_fusion.5
  166.1 2.5 fusion.122
  171.0 2.7 select_add_fusion.5
  173.8 2.5 fusion.122
  178.8 2.7 select_add_fusion.5
  181.6 2.5 fusion.122
  186.6 2.7 select_add_fusion.5
  189.3 2.5 fusion.122
  194.3 2.7 select_add_fusion.5
  197.1 2.5 fusion.122
  202.1 2.8 select_add_fusion.5
  204.8 2.5 fusion.122
  212.3 27.8 %while.80 = (s32[]{:T(128)}, f32[128,39,39]{0,2,1:T(8,128)}, f32[6,39,256]{2,1,0:T(8,128)S(1)}, f32[6,39,256]{2,1,0:T(8,128)}, bf16[6,128,256]{1,2,0:T(8,128)(2,...) while((s32[]{:T(128)}, f32[128,39,39]{0,2,1:T(8,128)}, ...), condition=%wide.region_23.24_spmd.clone, body=%wide.region_20.23_spmd.clone.sunk | while | flops 202076160 | bytes 2577003 | solution.py:44
  249.6 2.6 copy.79
  259.5 5.1 %all-to-all-start.1 = ((bf16[4,2,7680]{2,1,0:T(2,128)(2,1)}), bf16[4,2,7680]{2,1,0:T(2,128)(2,1)S(1)}, u32[]{:S(2)}, u32[]{:S(2)}) async-start(bf16[4,2,7680]{2,1,0:T(2,128)(2,1)} %reshape.220), calls=%async_computation.1 | async-start | bytes 245760 | tf_op jit(solution)/shard_map/all_to_all | solution.py:131
  264.6 6.6 %reduce-scatter.10.cloned.1.call-done = bf16[32,1521]{1,0:T(8,128)(2,1)} async-done(((bf16[128,1521]{1,0:T(8,128)(2,1)}), bf16[32,1521]{1,0:T(8,128)(2,1)}) %reduce-scatter.10.cloned.1.call-update) | async-done | bytes 97360
  273.1 30.4 %reduce-scatter.12.cloned.1.call-done = bf16[32,4992]{1,0:T(8,128)(2,1)} async-done(((bf16[128,4992]{1,0:T(8,128)(2,1)}), bf16[32,4992]{1,0:T(8,128)(2,1)}) %reduce-scatter.12.cloned.1.call-update) | async-done | bytes 319504
  305.7 30.0 %reduce-scatter.14.cloned.1.call-done = bf16[32,4992]{1,0:T(8,128)(2,1)} async-done(((bf16[128,4992]{1,0:T(8,128)(2,1)}), bf16[32,4992]{1,0:T(8,128)(2,1)}) %reduce-scatter.14.cloned.1.call-update) | async-done | bytes 319504
  340.9 71.5 %all-reduce.4.cloned.1.call-done = (bf16[32,1521]{0,1:T(8,128)(2,1)}, bf16[32,4992]{0,1:T(8,128)(2,1)}, bf16[32,4992]{0,1:T(8,128)(2,1)}) async-done(((bf16[32,1521]{0,1:T(8,128)(2,1)}, bf16[32,4992]{0,1:T(8,128)(2,1)}, bf16[32,4992]{0,1:T(8,128)(2,1)}), (bf16[32,1521]{0,1:T(8,128)(2,1)}, bf16[32,4992]{0,1:T(8,128)(2,1)}, bf16[32,4992]{0,1:T(8,128)(2,1)})) %all-reduce.4.cloned.1.call-update) | async-done | bytes 736336 | tf_op jit(solution)/shard_map/psum | solution.py:148
  (281 shorter events, 144.3 us)
Async XLA Ops:
  7.2 1.0 copy-start
  8.1 1.5 copy-start.13
  10.8 18.9 %all-to-all-start = ((bf16[4,2,7680]{2,1,0:T(2,128)(2,1)}), bf16[4,2,7680]{2,1,0:T(2,128)(2,1)S(1)}, u32[]{:S(2)}, u32[]{:S(2)}) async-start(bf16[4,2,7680]{2,1,0:T(2,128)(2,1)} %reshape.218), calls=%async_computation | async-start | bytes 245760 | tf_op jit(solution)/shard_map/all_to_all | solution.py:74
  17.1 254.1 %reduce-scatter.10.cloned.1.call-start = ((), (), s32[]{:S(2)}) async-start(), calls=%async_computation.5 | async-start | bytes 491520
  25.5 3.3 copy-start.10
  25.5 4.2 copy-start.12
  27.4 2.6 copy-start.15
  65.0 30.9 %copy-start.17 = (s32[24]{0:T(128)S(1)}, s32[24]{0:T(128)}, u32[]{:S(2)}) copy-start(s32[24]{0:T(128)} %param.23) | copy-start | bytes 292
  100.4 3.4 copy-start.3
  109.7 4.4 %copy-start.3 = (bf16[128,128,39]{0,1,2:T(8,128)(2,1)S(1)}, bf16[128,128,39]{0,1,2:T(8,128)(2,1)}, u32[]{:S(2)}) copy-start(bf16[128,128,39]{0,1,2:T(8,128)(2,1)} %get-tuple-element.813) | copy-start | bytes 3833860 | tf_op jit(solution)/shard_map/while
  119.8 4.4 %copy-start.3 = (bf16[128,128,39]{0,1,2:T(8,128)(2,1)S(1)}, bf16[128,128,39]{0,1,2:T(8,128)(2,1)}, u32[]{:S(2)}) copy-start(bf16[128,128,39]{0,1,2:T(8,128)(2,1)} %get-tuple-element.813) | copy-start | bytes 3833860 | tf_op jit(solution)/shard_map/while
  130.0 4.4 %copy-start.3 = (bf16[128,128,39]{0,1,2:T(8,128)(2,1)S(1)}, bf16[128,128,39]{0,1,2:T(8,128)(2,1)}, u32[]{:S(2)}) copy-start(bf16[128,128,39]{0,1,2:T(8,128)(2,1)} %get-tuple-element.813) | copy-start | bytes 3833860 | tf_op jit(solution)/shard_map/while
  140.2 4.4 %copy-start.3 = (bf16[128,128,39]{0,1,2:T(8,128)(2,1)S(1)}, bf16[128,128,39]{0,1,2:T(8,128)(2,1)}, u32[]{:S(2)}) copy-start(bf16[128,128,39]{0,1,2:T(8,128)(2,1)} %get-tuple-element.813) | copy-start | bytes 3833860 | tf_op jit(solution)/shard_map/while
  150.3 4.4 %copy-start.3 = (bf16[128,128,39]{0,1,2:T(8,128)(2,1)S(1)}, bf16[128,128,39]{0,1,2:T(8,128)(2,1)}, u32[]{:S(2)}) copy-start(bf16[128,128,39]{0,1,2:T(8,128)(2,1)} %get-tuple-element.813) | copy-start | bytes 3833860 | tf_op jit(solution)/shard_map/while
  163.3 2.8 copy-start.2
  171.0 2.8 copy-start.2
  178.8 2.8 copy-start.2
  186.6 2.8 copy-start.2
  194.3 2.8 copy-start.2
  202.0 2.8 copy-start.2
  240.1 0.7 copy-start.5
  244.9 58.6 %reduce-scatter.12.cloned.1.call-start = ((), (), s32[]{:S(2)}) async-start(), calls=%async_computation.6 | async-start | bytes 1597440
  249.6 2.7 copy-start.1
  252.2 83.5 %reduce-scatter.14.cloned.1.call-start = ((), (), s32[]{:S(2)}) async-start(), calls=%async_computation.7 | async-start | bytes 1597440
  256.1 2.0 copy-start.6
  256.2 2.0 copy-start.7
  256.2 2.0 copy-start.8
  256.2 2.0 copy-start.9
  256.2 2.2 copy-start.16
  259.5 78.5 %all-to-all-start.1 = ((bf16[4,2,7680]{2,1,0:T(2,128)(2,1)}), bf16[4,2,7680]{2,1,0:T(2,128)(2,1)S(1)}, u32[]{:S(2)}, u32[]{:S(2)}) async-start(bf16[4,2,7680]{2,1,0:T(2,128)(2,1)} %reshape.220), calls=%async_computation.1 | async-start | bytes 245760 | tf_op jit(solution)/shard_map/all_to_all | solution.py:131
  264.6 147.7 %all-reduce.4.cloned.1.call-start = ((), (), s32[]{:S(2)}) async-start(), calls=%async_computation.8 | async-start | bytes 5894144 | tf_op jit(solution)/shard_map/psum | solution.py:148
  338.0 0.7 copy-start.14
  412.3 2.4 copy-start.4
  412.3 4.1 copy-start.11
Sparse Core Ops, SparseCore 0:
  245.0 26.1 reduce-scatter.9
  274.1 29.2 reduce-scatter.11
  306.4 29.2 reduce-scatter.13
  338.8 73.5 all-reduce.3
where the time goes:
time: 427 us; the launch traced here: 424 us
  matrix products  151 us (35%)
  waiting for transfers between devices  139 us (33%)
  local copies, waits for them, and re-layouts  86.5 us (20%)
  other arithmetic  17.9 us (4%)
  between operations  14.1 us (3%)
  starting transfers between devices  11.5 us (3%)
    psum x1, waiting for transfers between devices, local(): lax.psum(shares[0].astype(jnp.bfloat16), ('samp', 'col'))  71.5 us
    unnamed x7, waiting for transfers between devices  67.1 us
    dot_general x18, matrix products, accumulate(): jnp.einsum('ol,cfl->ocf', cotangent_part, outer_products, preferred_eleme...  56.2 us
    dot_general x18, matrix products, one_block(): jnp.einsum('ocf,cfl->ol', filter_cube, outer_products, preferred_element_...  50.2 us
    dot_general x18, matrix products, accumulate(): jnp.einsum('ocf,ol->cfl', filter_cube, cotangent_part, preferred_element_...  39.7 us
    dynamic_update_slice x42, local copies, waits for them, and re-layouts, backward_layer(): lax.scan(accumulate, starting, (cotangent, previous, anchor))  31.1 us
    unnamed x49, local copies, waits for them, and re-layouts  27 us
  transfers between devices with their start and end apart: 6, of which 4 were waited for; matrix products, arithmetic and copies ran while one was open for 8% of the time, Pallas kernels for 0%

commit v1 on v0

--- a/solution.py
+++ b/solution.py
@@ -145,7 +145,9 @@
         ).astype(jnp.float32),
     )
     summed = (
-        lax.psum(shares[0].astype(jnp.bfloat16), ("samp", "col")).astype(jnp.float32),
+        jax.lax.psum(jax.lax.psum(shares[0].astype(jnp.bfloat16), "col"), "samp").astype(
+            jnp.float32
+        ),
         lax.psum(shares[1].astype(jnp.bfloat16), ("samp", "col")).astype(jnp.float32),
         lax.psum(shares[2].astype(jnp.bfloat16), ("samp", "col")).astype(jnp.float32),
     )

time: 427 us -> 482 us (1.13)
  waiting for transfers between devices: 139 us -> 191 us
    psum x1 -> x3, waiting for transfers between devices: 71.5 us -> 107 us  [the longest x1 68.7 us: local(): lax.psum(shares[1].astype(jnp.bfloat16), ('samp', 'col'))]
    unnamed x7 -> x9, waiting for transfers between devices: 67.1 us -> 83.7 us
    unnamed x49 -> x47, local copies, waits for them, and re-layouts: 27 us -> 28.3 us
  transfers between devices with their start and end apart: 6 -> 8, of which waited for: 4 -> 6; matrix products, arithmetic and copies ran while one was open for 8% -> 8% of each run, Pallas kernels for 0% -> 0%
where the time goes in v1:
time: 482 us; the launch traced here: 478 us
  waiting for transfers between devices  191 us (40%)
  matrix products  149 us (31%)
  local copies, waits for them, and re-layouts  91.1 us (19%)
  other arithmetic  16.4 us (3%)
  between operations  14.4 us (3%)
  starting transfers between devices  11.4 us (2%)
    unnamed x9, waiting for transfers between devices  83.7 us
    psum x1, waiting for transfers between devices, local(): lax.psum(shares[1].astype(jnp.bfloat16), ('samp', 'col'))  68.7 us
    dot_general x18, matrix products, accumulate(): jnp.einsum('ol,cfl->ocf', cotangent_part, outer_products, preferred_eleme...  55.1 us
    dot_general x18, matrix products, one_block(): jnp.einsum('ocf,cfl->ol', filter_cube, outer_products, preferred_element_...  50 us
    dot_general x18, matrix products, accumulate(): jnp.einsum('ocf,ol->cfl', filter_cube, cotangent_part, preferred_element_...  39.5 us
    psum x1, waiting for transfers between devices, local(): jax.lax.psum(jax.lax.psum(shares[0].astype(jnp.bfloat16), 'col'), 'samp')  34.2 us
    dynamic_update_slice x42, local copies, waits for them, and re-layouts, backward_layer(): lax.scan(accumulate, starting, (cotangent, previous, anchor))  31.1 us
    unnamed x47, local copies, waits for them, and re-layouts  28.3 us
  transfers between devices with their start and end apart: 8, of which 6 were waited for; matrix products, arithmetic and copies ran while one was open for 8% of the time, Pallas kernels for 0%

profile of v1, /device:TPU:0, one launch (start us, length us, event | category | flops | bytes accessed | tf_op | source)
XLA Modules:
  0.0 478.1 jit_solution(12594845597933459920)
XLA Ops:
  10.8 6.3 %all-to-all-start = ((bf16[4,2,7680]{2,1,0:T(2,128)(2,1)}), bf16[4,2,7680]{2,1,0:T(2,128)(2,1)S(1)}, u32[]{:S(2)}, u32[]{:S(2)}) async-start(bf16[4,2,7680]{2,1,0:T(2,128)(2,1)} %reshape.218), calls=%async_computation | async-start | bytes 245760 | tf_op jit(solution)/shard_map/all_to_all | solution.py:74
  33.9 9.0 %while.75 = (s32[]{:T(128)}, bf16[6,128,256]{1,2,0:T(8,128)(2,1)S(1)}, bf16[6,39,256]{2,1,0:T(8,128)(2,1)S(1)}, bf16[128,39,39]{0,2,1:T(8,128)(2,1)}, s32[]{:T(128)}) while((s32[]{:T(128)}, bf16[6,128,256]{1,2,0:T(8,128)(2,1)S(1)}, bf16[6,39,256]{2,1,0:T(8,128)(2,1)S(1)}, bf16[128,39,39]{0,2,1:T(8,128)(2,1)}, s32[]{:T(128)}) %tuple.131), condition=%wide.region_1.2_spmd, body=%wide.region_0.1_spmd.sunk | while | flops 100501760 | bytes 596805 | solution.py:25
  43.8 20.9 %while.76 = (s32[]{:T(128)}, bf16[6,128,256]{1,2,0:T(8,128)(2,1)}, bf16[6,128,256]{1,2,0:T(8,128)(2,1)S(1)}, bf16[6,39,256]{2,1,0:T(8,128)(2,1)S(1)}, bf16[128,128,39]{1,0,2:T(8,128)(2,1)}, /*index=5*/s32[]{:T(128)}) while((s32[]{:T(128)}, bf16[6,128,256]{1,2,0:T(8,128)(2,1)}, bf16[6,128,256]{1,2,0:T(8,128)(2,1)S(1)}, ...), condition=%wide.region_5.6_spmd, body=%wide.region_4.5_spmd.sunk | while | flops 329787136 | bytes 1771597 | solution.py:25
  43.8 3.4 fusion.114
  47.3 3.4 fusion.114
  50.8 3.4 fusion.114
  54.3 3.4 fusion.114
  57.7 3.4 fusion.114
  61.2 3.4 fusion.114
  66.6 25.9 %while.77 = (s32[]{:T(128)}, bf16[6,128,256]{1,2,0:T(8,128)(2,1)}, bf16[6,128,256]{1,2,0:T(8,128)(2,1)}, bf16[6,39,256]{2,1,0:T(8,128)(2,1)S(1)}, bf16[128,128,39]{1,0,2:T(8,128)(2,1)}, /*index=5*/s32[]{:T(128)}) while((s32[]{:T(128)}, bf16[6,128,256]{1,2,0:T(8,128)(2,1)}, bf16[6,128,256]{1,2,0:T(8,128)(2,1)}, ...), condition=%wide.region_9.10_spmd, body=%wide.region_8.9_spmd.sunk | while | flops 329787136 | bytes 1771597 | solution.py:25
  67.4 3.4 fusion.116
  71.7 3.4 fusion.116
  76.1 3.4 fusion.116
  80.4 3.4 fusion.116
  84.7 3.4 fusion.116
  89.0 3.4 fusion.116
  93.5 3.7 all-reduce
  100.8 60.1 %while.78 = (s32[]{:T(128)}, f32[128,128,39]{1,0,2:T(8,128)}, f32[6,128,256]{1,2,0:T(8,128)}, f32[6,39,256]{2,1,0:T(8,128)}, bf16[6,128,256]{1,2,0:T(8,128)(2,1)...) while((s32[]{:T(128)}, f32[128,128,39]{1,0,2:T(8,128)}, ...), condition=%wide.region_15.16_spmd.clone, body=%wide.region_12.15_spmd.clone.sunk | while | flops 663257088 | bytes 13271699 | solution.py:44
  101.9 3.4 select_add_fusion.4
  111.1 4.3 select_add_fusion.4
  121.3 4.3 select_add_fusion.4
  131.4 4.3 select_add_fusion.4
  135.8 2.5 fusion.119
  141.6 4.3 select_add_fusion.4
  145.9 2.5 fusion.119
  151.8 4.3 select_add_fusion.4
  156.1 2.5 fusion.119
  164.5 46.5 %while.79 = (s32[]{:T(128)}, f32[128,128,39]{1,0,2:T(8,128)S(1)}, f32[6,128,256]{1,2,0:T(8,128)}, f32[6,39,256]{2,1,0:T(8,128)}, bf16[6,128,256]{1,2,0:T(8,128)(...) while((s32[]{:T(128)}, f32[128,128,39]{1,0,2:T(8,128)S(1)}, ...), condition=%wide.region_19.20_spmd.clone, body=%wide.region_16.19_spmd.clone.sunk | while | flops 663257088 | bytes 13271699 | solution.py:44
  164.7 2.8 select_add_fusion.5
  167.5 2.5 fusion.122
  172.4 2.8 select_add_fusion.5
  175.2 2.5 fusion.122
  180.2 2.7 select_add_fusion.5
  183.0 2.5 fusion.122
  188.0 2.8 select_add_fusion.5
  190.7 2.5 fusion.122
  195.7 2.7 select_add_fusion.5
  203.4 2.7 select_add_fusion.5
  206.2 2.5 fusion.122
  213.7 26.6 %while.80 = (s32[]{:T(128)}, f32[128,39,39]{0,2,1:T(8,128)}, f32[6,39,256]{2,1,0:T(8,128)}, f32[6,39,256]{2,1,0:T(8,128)}, bf16[6,128,256]{1,2,0:T(8,128)(2,1)S(...) while((s32[]{:T(128)}, f32[128,39,39]{0,2,1:T(8,128)}, ...), condition=%wide.region_23.24_spmd.clone, body=%wide.region_20.23_spmd.clone.sunk | while | flops 202076160 | bytes 2543987 | solution.py:44
  244.4 26.3 %reduce-scatter.10.cloned.1.call-done = bf16[32,1521]{1,0:T(8,128)(2,1)} async-done(((bf16[128,1521]{1,0:T(8,128)(2,1)}), bf16[32,1521]{1,0:T(8,128)(2,1)}) %reduce-scatter.10.cloned.1.call-update) | async-done | bytes 97360
  277.3 2.6 copy.79
  287.5 4.5 all-reduce.6.cloned.1.call-done
  293.2 4.9 %all-to-all-start.1 = ((bf16[4,2,7680]{2,1,0:T(2,128)(2,1)}), bf16[4,2,7680]{2,1,0:T(2,128)(2,1)S(1)}, u32[]{:S(2)}, u32[]{:S(2)}) async-start(bf16[4,2,7680]{2,1,0:T(2,128)(2,1)} %reshape.220), calls=%async_computation.1 | async-start | bytes 245760 | tf_op jit(solution)/shard_map/all_to_all | solution.py:131
  298.1 27.4 %reduce-scatter.12.cloned.1.call-done = bf16[32,4992]{1,0:T(8,128)(2,1)} async-done(((bf16[128,4992]{1,0:T(8,128)(2,1)}), bf16[32,4992]{1,0:T(8,128)(2,1)}) %reduce-scatter.12.cloned.1.call-update) | async-done | bytes 319504
  327.7 29.9 %reduce-scatter.14.cloned.1.call-done = bf16[32,4992]{1,0:T(8,128)(2,1)} async-done(((bf16[128,4992]{1,0:T(8,128)(2,1)}), bf16[32,4992]{1,0:T(8,128)(2,1)}) %reduce-scatter.14.cloned.1.call-update) | async-done | bytes 319504
  362.5 34.2 %all-reduce.8.cloned.1.call-done = bf16[32,1521]{0,1:T(8,128)(2,1)} async-done(((bf16[32,1521]{0,1:T(8,128)(2,1)}), bf16[32,1521]{0,1:T(8,128)(2,1)}) %all-reduce.8.cloned.1.call-update) | async-done | bytes 97360 | tf_op jit(solution)/shard_map/psum | solution.py:148
  398.5 68.7 %all-reduce.10.cloned.1.call-done = (bf16[32,4992]{0,1:T(8,128)(2,1)}, bf16[32,4992]{0,1:T(8,128)(2,1)}) async-done(((bf16[32,4992]{0,1:T(8,128)(2,1)}, bf16[32,4992]{0,1:T(8,128)(2,1)}), (bf16[32,4992]{0,1:T(8,128)(2,1)}, bf16[32,4992]{0,1:T(8,128)(2,1)})) %all-reduce.10.cloned.1.call-update) | async-done | bytes 638992 | tf_op jit(solution)/shard_map/psum | solution.py:151
  (285 shorter events, 151.2 us)
Async XLA Ops:
  7.2 1.0 copy-start
  8.1 1.5 copy-start.12
  8.1 9.0 %copy-start.2 = (bf16[128,4992]{1,0:T(8,128)(2,1)S(1)}, bf16[128,4992]{1,0:T(8,128)(2,1)}, u32[]{:S(2)}) copy-start(bf16[128,4992]{1,0:T(8,128)(2,1)} %param.27) | copy-start | bytes 3833860
  10.8 22.2 %all-to-all-start = ((bf16[4,2,7680]{2,1,0:T(2,128)(2,1)}), bf16[4,2,7680]{2,1,0:T(2,128)(2,1)S(1)}, u32[]{:S(2)}, u32[]{:S(2)}) async-start(bf16[4,2,7680]{2,1,0:T(2,128)(2,1)} %reshape.218), calls=%async_computation | async-start | bytes 245760 | tf_op jit(solution)/shard_map/all_to_all | solution.py:74
  17.1 253.5 %reduce-scatter.10.cloned.1.call-start = ((), (), s32[]{:S(2)}) async-start(), calls=%async_computation.7 | async-start | bytes 491520
  28.8 3.3 copy-start.10
  28.8 4.2 copy-start.11
  30.7 2.6 copy-start.14
  66.6 30.9 %copy-start.16 = (s32[24]{0:T(128)S(1)}, s32[24]{0:T(128)}, u32[]{:S(2)}) copy-start(s32[24]{0:T(128)} %param.23) | copy-start | bytes 292
  101.9 3.4 copy-start.4
  111.1 4.3 copy-start.4
  121.3 4.3 copy-start.4
  131.4 4.3 copy-start.4
  141.6 4.3 copy-start.4
  151.7 4.3 copy-start.4
  164.7 2.8 copy-start.3
  172.4 2.8 copy-start.3
  180.2 2.8 copy-start.3
  188.0 2.8 copy-start.3
  195.7 2.8 copy-start.3
  203.4 2.8 copy-start.3
  244.3 47.7 %all-reduce.6.cloned.1.call-start = ((), (), s32[]{:S(2)}) async-start(), calls=%async_computation.5 | async-start | bytes 782336 | tf_op jit(solution)/shard_map/psum | solution.py:148
  272.5 52.9 %reduce-scatter.12.cloned.1.call-start = ((), (), s32[]{:S(2)}) async-start(), calls=%async_computation.8 | async-start | bytes 1597440
  277.3 2.7 copy-start.1
  279.9 77.7 %reduce-scatter.14.cloned.1.call-start = ((), (), s32[]{:S(2)}) async-start(), calls=%async_computation.9 | async-start | bytes 1597440
  284.7 2.6 copy-start.6
  284.7 2.6 copy-start.7
  284.7 2.6 copy-start.8
  284.7 2.6 copy-start.9
  284.7 7.4 %copy-start.15 = (s32[40]{0:T(128)S(1)}, s32[40]{0:T(128)}, u32[]{:S(2)}) copy-start(s32[40]{0:T(128)} %param.22) | copy-start | bytes 484
  287.2 109.4 %all-reduce.8.cloned.1.call-start = ((), (), s32[]{:S(2)}) async-start(), calls=%async_computation.6 | async-start | bytes 782336 | tf_op jit(solution)/shard_map/psum | solution.py:148
  293.2 66.7 %all-to-all-start.1 = ((bf16[4,2,7680]{2,1,0:T(2,128)(2,1)}), bf16[4,2,7680]{2,1,0:T(2,128)(2,1)S(1)}, u32[]{:S(2)}, u32[]{:S(2)}) async-start(bf16[4,2,7680]{2,1,0:T(2,128)(2,1)} %reshape.220), calls=%async_computation.1 | async-start | bytes 245760 | tf_op jit(solution)/shard_map/all_to_all | solution.py:131
  298.1 169.1 %all-reduce.10.cloned.1.call-start = ((), (), s32[]{:S(2)}) async-start(), calls=%async_computation.10 | async-start | bytes 5111808 | tf_op jit(solution)/shard_map/psum | solution.py:151
  327.7 32.6 %copy-start.13 = (s32[1920]{0:T(1024)S(1)}, s32[1920]{0:T(1024)}, u32[]{:S(2)}) copy-start(s32[1920]{0:T(1024)} %copy-done.12) | copy-start | bytes 23044
  467.2 2.4 copy-start.5
Sparse Core Ops, SparseCore 0:
  244.5 26.1 reduce-scatter.9
  273.6 18.3 all-reduce.5
  295.0 30.4 reduce-scatter.11
  328.3 29.2 reduce-scatter.13
  359.8 36.8 all-reduce.7
  399.0 68.1 all-reduce.9
